TPU v7x, 256 devices: a whole 4x4x8 slice. The times are simulated.
256 devices in a mesh: asset: 16 (over y, x_hi, core), tm: 16 (over z, x_lo).
Axes of the slice: x: 4 (x_hi: 2, x_lo: 2; x = x_hi * 2 + x_lo), y: 4, z: 8, core: 2. Of those that a mesh axis runs over, the one named last changes fastest.
Arguments:
- day_ranks: int32 [224, 4096], P('tm', 'asset'), may hold values from 2 to 240
- confidence: float32 [224, 4096], P('tm', 'asset'), may hold values from 0.25 to 4
Outputs:
- correlation: bfloat16 [96, 4096, 4096], P('tm', 'asset')
All inputs are finite; a program needn't handle non-finite values.
Results may differ from a plain program's by a relative error of at most 0.001.
Values sent between devices are 32-bit elements; how exact they have to be, the bound alone decides.
A program may use at most 64 MiB of HBM per device.

v0:
```python
import jax
import jax.numpy as jnp
from jax import lax
from jax.sharding import PartitionSpec as P

WIN = 120
ENDS_DEV = 6
SPAN = 125


epsilon = 1e-06


def copy_for_each(shard, axis):
    size = lax.axis_size(axis)
    return lax.all_to_all(
        jnp.broadcast_to(shard[None], (size, *shard.shape)), axis, 0, 0, tiled=True
    )


def joined_along(tiles, dim):
    shape = list(tiles.shape[1:])
    shape[dim] *= tiles.shape[0]
    return jnp.moveaxis(tiles, 0, dim).reshape(shape)


def gathered_copies(shard, axis, dim):
    tiles = copy_for_each(shard, axis)
    return joined_along(tiles, dim)


def window_moments(span_rows):
    windows = jnp.stack([span_rows[offset : offset + WIN] for offset in range(ENDS_DEV)])
    window_mean = jnp.sum(windows, 1) / WIN
    centred = windows - window_mean[:, None, :]
    window_scale = lax.rsqrt(jnp.sum(centred * centred, 1) / WIN + epsilon)
    return (window_mean, window_scale)


def window_gram(left_rows, right_rows, start_index, stop_index):
    return lax.dot_general(
        left_rows[start_index:stop_index],
        right_rows[start_index:stop_index],
        (((0,), (0,)), ((), ())),
        precision=lax.Precision.HIGHEST,
        preferred_element_type=jnp.float32,
    )


def cross_tile(own_span, own_moments, other_span):
    other_mean, other_scale = window_moments(other_span)
    own_mean, own_scale = own_moments
    gram_sums = jnp.stack(
        [window_gram(own_span, other_span, offset, offset + WIN) for offset in range(ENDS_DEV)]
    )
    centre = own_mean[:, :, None] * other_mean[:, None, :]
    spread = own_scale[:, :, None] * other_scale[:, None, :]
    return ((gram_sums / WIN - centre) * spread).astype(jnp.bfloat16)


def per_device(day_ranks, confidence):
    days_dev = day_ranks.shape[0]
    time_count = lax.axis_size("tm")
    lead_days = days_dev * time_count - ENDS_DEV * time_count - WIN + 1
    scores = confidence * (day_ranks - (WIN + 1)).astype(jnp.float32) / WIN
    all_days = gathered_copies(scores, "tm", 0)
    first_day = lead_days + lax.axis_index("tm") * ENDS_DEV
    own_span = lax.dynamic_slice_in_dim(all_days, first_day, SPAN, 0)
    own_moments = window_moments(own_span)
    return cross_tile(own_span, own_moments, lax.all_gather(own_span, "asset", axis=1, tiled=True))


def solution(mesh):
    return jax.shard_map(
        per_device,
        mesh=mesh,
        in_specs=(P("tm", "asset"), P("tm", "asset")),
        out_specs=P("tm", "asset", None),
        check_vma=False,
    )
```

profile of v0, /device:TPU:1, one launch (start us, length us, event | category | flops | bytes accessed | tf_op | source)
XLA Modules:
  0.0 140.8 jit_solution(17189027588636391859)
XLA Ops:
  6.5 0.7 multiply_multiply_fusion
  7.3 0.7 broadcast_in_dim.2
  8.0 10.0 %all-to-all-start = ((f32[16,14,256]{2,1,0:T(8,128)}), f32[16,14,256]{2,1,0:T(8,128)S(1)}, u32[]{:S(2)}, u32[]{:S(2)}) async-start(f32[16,14,256]{2,1,0:T(8,128)} %broadcast_in_dim.2), calls=%async_computation | async-start | bytes 524288 | tf_op jit(solution)/shard_map/all_to_all | solution.py:16
  18.0 0.0 all-gather.2.cloned.1.call-start
  18.1 10.5 %all-to-all-done = f32[16,14,256]{2,1,0:T(8,128)S(1)} async-done(((f32[16,14,256]{2,1,0:T(8,128)}), f32[16,14,256]{2,1,0:T(8,128)S(1)}, u32[]{:S(2)}, u32[]{:S(2)}) %all-to-all-start) | async-done | bytes 229408 | tf_op jit(solution)/shard_map/all_to_all | solution.py:16
  28.7 0.7 constant_dynamic-slice_fusion
  29.3 0.0 all-gather.2.cloned.1.call-update
  29.5 0.1 reduce_sum.36
  29.6 0.1 multiply_reduce_fusion.1
  29.7 50.5 %all-gather.2.cloned.1.call-done = f32[125,4096]{1,0:T(8,128)} async-done(((f32[125,256]{1,0:T(8,128)}), f32[125,4096]{1,0:T(8,128)}) %all-gather.2.cloned.1.call-update) | async-done | bytes 2048016 | tf_op jit(solution)/shard_map/all_gather | solution.py:70
  80.2 0.0 copy-start
  80.2 3.1 %bitcast_dynamic-update-slice_fusion.5 = f32[6,120,4096]{2,1,0:T(8,128)} fusion(f32[125,4096]{1,0:T(8,128)} %all-gather.2.cloned.1.call-done), kind=kLoop, calls=%fused_computation.19 | loop fusion | bytes 3932160
  83.4 3.0 %bitcast_dynamic-update-slice_fusion.4 = f32[6,120,4096]{2,1,0:T(8,128)} fusion(f32[6,120,4096]{2,1,0:T(8,128)} %bitcast_dynamic-update-slice_fusion.5, f32[125,4096]{1,0:T(8,128)} %all-gather.2.cloned.1.call-done), kind=kLoop, calls=%fused_computation.18 | loop fusion | bytes 3932160
  86.4 3.0 %bitcast_dynamic-update-slice_fusion.3 = f32[6,120,4096]{2,1,0:T(8,128)} fusion(f32[6,120,4096]{2,1,0:T(8,128)} %bitcast_dynamic-update-slice_fusion.4, f32[125,4096]{1,0:T(8,128)} %all-gather.2.cloned.1.call-done), kind=kLoop, calls=%fused_computation.17 | loop fusion | bytes 3932160
  89.4 0.0 copy-done
  89.4 1.4 %bitcast_dynamic-update-slice_fusion.2 = f32[6,120,4096]{2,1,0:T(8,128)} fusion(f32[6,120,4096]{2,1,0:T(8,128)} %bitcast_dynamic-update-slice_fusion.3, f32[125,4096]{1,0:T(8,128)S(1)} %copy-done), kind=kLoop, calls=%fused_computation.16 | loop fusion | bytes 3932160
  90.8 1.4 %bitcast_dynamic-update-slice_fusion.1 = f32[6,120,4096]{2,1,0:T(8,128)} fusion(f32[6,120,4096]{2,1,0:T(8,128)} %bitcast_dynamic-update-slice_fusion.2, f32[125,4096]{1,0:T(8,128)S(1)} %copy-done), kind=kLoop, calls=%fused_computation.15 | loop fusion | bytes 3932160
  92.3 1.4 %bitcast_dynamic-update-slice_fusion = f32[6,120,4096]{2,1,0:T(8,128)} fusion(f32[6,120,4096]{2,1,0:T(8,128)} %bitcast_dynamic-update-slice_fusion.1, f32[125,4096]{1,0:T(8,128)S(1)} %copy-done), kind=kLoop, calls=%fused_computation.14 | loop fusion | bytes 3932160 | tf_op jit(solution)/shard_map/stack | solution.py:33
  93.7 5.2 %reduce_sum.37 = f32[6,4096]{1,0:T(8,128)S(1)} reduce(f32[6,120,4096]{2,1,0:T(8,128)} %bitcast_dynamic-update-slice_fusion, f32[]{:T(128)} %constant.30.clone.1), dimensions={1}, to_apply=%region_1.0 | reduce | flops 2924544 | bytes 11894788 | tf_op jit(solution)/shard_map/reduce_sum | solution.py:34
  98.9 6.0 %multiply_reduce_fusion = f32[6,4096]{1,0:T(8,128)S(1)} fusion(f32[6,120,4096]{2,1,0:T(8,128)} %bitcast_dynamic-update-slice_fusion, f32[6,4096]{1,0:T(8,128)S(1)} %broadcast_multiply_fusion), kind=kLoop, calls=%fused_computation.1 | loop fusion | flops 8822784 | bytes 11993088 | tf_op jit(solution)/shard_map/reduce_sum | solution.py:36
  104.9 3.5 %fusion.5 = f32[6,256,4096]{2,1,0:T(8,128)S(1)} fusion(f32[125,4096]{1,0:T(8,128)S(1)} %copy-done, f32[224,256]{1,0:T(8,128)S(1)} %reshape.23, s32[]{:T(128)S(6)} %select_n.3), kind=kOutput, calls=%fused_computation.13 | convolution fusion | flops 1509949440 | bytes 6283268 | tf_op jit(solution)/shard_map/dot_general | solution.py:41
  108.5 3.5 %fusion.4 = f32[6,256,4096]{2,1,0:T(8,128)S(1)} fusion(f32[6,256,4096]{2,1,0:T(8,128)S(1)} %fusion.5, f32[125,4096]{1,0:T(8,128)S(1)} %copy-done, f32[224,256]{1,0:T(8,128)S(1)} %reshape.23, s32[]{:T(128)S(6)} %add.31), kind=kOutput, calls=%fused_computation.11 | convolution fusion | flops 1509949440 | bytes 6283268 | tf_op jit(solution)/shard_map/dot_general | solution.py:41
  112.0 3.7 %fusion.3 = f32[6,256,4096]{2,1,0:T(8,128)S(1)} fusion(f32[6,256,4096]{2,1,0:T(8,128)S(1)} %fusion.4, f32[125,4096]{1,0:T(8,128)S(1)} %copy-done, f32[224,256]{1,0:T(8,128)S(1)} %reshape.23, s32[]{:T(128)S(6)} %add.32), kind=kOutput, calls=%fused_computation.9 | convolution fusion | flops 1509949440 | bytes 6283268 | tf_op jit(solution)/shard_map/dot_general | solution.py:41
  115.7 3.5 %fusion.2 = f32[6,256,4096]{2,1,0:T(8,128)S(1)} fusion(f32[6,256,4096]{2,1,0:T(8,128)S(1)} %fusion.3, f32[125,4096]{1,0:T(8,128)S(1)} %copy-done, f32[224,256]{1,0:T(8,128)S(1)} %reshape.23, s32[]{:T(128)S(6)} %add.33), kind=kOutput, calls=%fused_computation.7 | convolution fusion | flops 1509949440 | bytes 6283268 | tf_op jit(solution)/shard_map/dot_general | solution.py:41
  119.2 3.5 %fusion.1 = f32[6,256,4096]{2,1,0:T(8,128)S(1)} fusion(f32[6,256,4096]{2,1,0:T(8,128)S(1)} %fusion.2, f32[125,4096]{1,0:T(8,128)S(1)} %copy-done, f32[224,256]{1,0:T(8,128)S(1)} %reshape.23, s32[]{:T(128)S(6)} %add.34), kind=kOutput, calls=%fused_computation.5 | convolution fusion | flops 1509949440 | bytes 6283268 | tf_op jit(solution)/shard_map/dot_general | solution.py:41
  122.7 3.5 %fusion = f32[6,256,4096]{2,1,0:T(8,128)S(1)} fusion(f32[6,256,4096]{2,1,0:T(8,128)S(1)} %fusion.1, f32[125,4096]{1,0:T(8,128)S(1)} %copy-done, f32[224,256]{1,0:T(8,128)S(1)} %reshape.23, s32[]{:T(128)S(6)} %add.35), kind=kOutput, calls=%fused_computation.3 | convolution fusion | flops 1509949440 | bytes 6283268 | tf_op jit(solution)/shard_map/dot_general | solution.py:41
  126.2 7.8 %multiply_convert_fusion = bf16[6,256,4096]{2,1,0:T(8,128)(2,1)} fusion(f32[6,256,4096]{2,1,0:T(8,128)S(1)} %fusion, f32[6,4096]{1,0:T(8,128)S(1)} %add_rsqrt_fusion, f32[6,256]{1,0:T(8,128)S(1)} %add_rsqrt_fusion.1, f32[6,4096]{1,0:T(8,128)S(1)} %broadcast_multiply_fusion, f32[6,256]{1,0:T(8,128)S(1)} %broadcast_multiply_fusion.1), kind=kLoop, calls=%fused_computation | loop fusion | flops 37748736 | bytes 37957632 | tf_op jit(solution)/shard_map/convert_element_type | solution.py:58
  (11 shorter events, 0.2 us)
Async XLA Ops:
  8.0 20.6 %all-to-all-start = ((f32[16,14,256]{2,1,0:T(8,128)}), f32[16,14,256]{2,1,0:T(8,128)S(1)}, u32[]{:S(2)}, u32[]{:S(2)}) async-start(f32[16,14,256]{2,1,0:T(8,128)} %broadcast_in_dim.2), calls=%async_computation | async-start | bytes 524288 | tf_op jit(solution)/shard_map/all_to_all | solution.py:16
  18.0 62.2 %all-gather.2.cloned.1.call-start = ((), (), s32[]{:S(2)}) async-start(), calls=%async_computation.1 | async-start | bytes 2228224 | tf_op jit(solution)/shard_map/all_gather | solution.py:70
  80.2 9.2 %copy-start = (f32[125,4096]{1,0:T(8,128)S(1)}, f32[125,4096]{1,0:T(8,128)}, u32[]{:S(2)}) copy-start(f32[125,4096]{1,0:T(8,128)} %all-gather.2.cloned.1.call-done) | copy-start | bytes 6144004
Sparse Core Ops, SparseCore 0:
  29.5 50.7 all-gather.1
where the time goes:
time: 141 us
  waiting for transfers between devices  61.1 us (43%)
  matrix products  21.3 us (15%)
  other arithmetic  19.9 us (14%)
  local copies, waits for them, and re-layouts  15 us (11%)
  between operations  13.6 us (10%)
  starting transfers between devices  10.1 us (7%)
    all_gather x1, waiting for transfers between devices, per_device(): lax.all_gather(own_span, 'asset', axis=1, tiled=True)  50.5 us
    dot_general x6, matrix products, window_gram(): lax.dot_general(left_rows[start_index:stop_index], right_rows[start_index...  21.3 us
    unnamed x12, local copies, waits for them, and re-layouts  12.1 us
    all_to_all x1, waiting for transfers between devices, copy_for_each(): lax.all_to_all(jnp.broadcast_to(shard[None], (size, *shard.shape)), axis,...  10.5 us
    all_to_all x1, starting transfers between devices, copy_for_each(): lax.all_to_all(jnp.broadcast_to(shard[None], (size, *shard.shape)), axis,...  10 us
    convert_element_type x1, other arithmetic, cross_tile(): return ((gram_sums / WIN - centre) * spread).astype(jnp.bfloat16)  7.76 us
    reduce_sum x2, other arithmetic, window_moments(): window_scale = lax.rsqrt(jnp.sum(centred * centred, 1) / WIN + epsilon)  6.09 us
    reduce_sum x2, other arithmetic, window_moments(): window_mean = jnp.sum(windows, 1) / WIN  5.24 us
  transfers between devices with their start and end apart: 2, of which 2 were waited for; matrix products, arithmetic and copies ran while one was open for 0% of the time, Pallas kernels for 0%

commit v1 on v0

v1 whole, which is shorter than its diff:
```python
import functools

import jax
import jax.numpy as jnp
from jax import lax
from jax.experimental import pallas as pl
from jax.experimental.pallas import tpu as pltpu
from jax.sharding import PartitionSpec as P

WIN = 120
ENDS_DEV = 6
SPAN = 125
LEAD = 9
HALF = 7
SLOTS = 10
PART = SLOTS * HALF
PIECES = 34
SEC = 144
DEPTH = 512
STOCKS = 256
BLOCKS = 16
epsilon = 1e-06
MESH = pl.DeviceIdType.MESH


def first_half(z):
    return jnp.minimum((LEAD + 12 * z) // HALF, 12)


def first_local(z, x_lo):
    g = first_half(z) - 2 * x_lo + 4
    return 2 * (g // 4 - 1) + jnp.minimum(g % 4, 2)


def gather_kernel(ranks_ref, conf_ref, g_ref, mine, zsend, zrecv, recv, send, csend, crecv):
    asset, tm = lax.axis_index("asset"), lax.axis_index("tm")
    core, x_hi, y = asset % 2, asset // 2 % 2, asset // 4
    z, x_lo = tm // 2, tm % 2
    x = x_hi * 2 + x_lo

    def chip(cx, cy):
        return ((cy * 2 + cx // 2) * 2 + core, z * 2 + cx % 2)

    def piece(cx, cy):
        return ((cy * 2 + cx // 2) * 2 + core) * 2 + cx % 2

    xs = [x, (x + 3) % 4, (x + 1) % 4, (x + 2) % 4]
    ys = [y, (y + 3) % 4, (y + 1) % 4, (y + 2) % 4]
    x_minus, x_plus = chip(xs[1], y), chip(xs[2], y)
    y_minus, y_plus = chip(x, ys[1]), chip(x, ys[2])
    partner = (asset + 1 - 2 * core, tm)
    line = [(asset, ((z + step) % 8) * 2 + x_lo) for step in range(1, 8)]

    barrier = pltpu.get_barrier_semaphore()
    for peer in line + [x_minus, x_plus, y_minus, y_plus, partner]:
        pl.semaphore_signal(barrier, inc=1, device_id=peer, device_id_type=MESH)

    scores = conf_ref[...] * (ranks_ref[...] - (WIN + 1)).astype(jnp.float32) / WIN
    for day in range(2 * HALF):
        for h in range(2):
            mine[day // HALF, day % HALF, h : h + 1, :] = scores[
                day : day + 1, h * 128 : (h + 1) * 128
            ]
    own = piece(x, y)
    first = first_local(z, x_lo)
    for b in range(2):
        slot = 2 * z + b - first

        @pl.when((slot >= 0) & (slot < SLOTS))
        def _():
            for day in range(HALF):
                for h in range(2):
                    g_ref[own, slot, day, h : h + 1, :] = scores[
                        b * HALF + day : b * HALF + day + 1, h * 128 : (h + 1) * 128
                    ]

    pl.semaphore_wait(barrier, 12)

    def z_copy(step, b):
        there = (z + step) % 8
        slot = 2 * z + b - first_local(there, x_lo)
        copy = pltpu.make_async_remote_copy(
            src_ref=mine.at[b],
            dst_ref=g_ref.at[own, jnp.clip(slot, 0, SLOTS - 1)],
            send_sem=zsend.at[2 * step + b],
            recv_sem=zrecv.at[jnp.clip(slot, 0, SLOTS - 1)],
            device_id=(asset, there * 2 + x_lo),
            device_id_type=MESH,
        )
        return (slot >= 0) & (slot < SLOTS), copy

    for step in (4, 3, 5, 2, 6, 1, 7):
        for b in range(2):
            go, copy = z_copy(step, b)
            pl.when(go)(copy.start)

    for slot in range(SLOTS):

        @pl.when((first + slot) // 2 != z)
        def _():
            pltpu.make_async_copy(mine.at[0], g_ref.at[own, slot], zrecv.at[slot]).wait()

    def part(cx, cy, low, high):
        return g_ref.at[piece(cx, cy), pl.ds(low, high - low)]

    def push(cx, cy, low, high, sem, peer):
        pltpu.make_async_remote_copy(
            src_ref=part(cx, cy, low, high),
            dst_ref=part(cx, cy, low, high),
            send_sem=send,
            recv_sem=recv.at[sem],
            device_id=peer,
            device_id_type=MESH,
        ).start()

    def arrived(cx, cy, low, high, sem):
        ref = part(cx, cy, low, high)
        pltpu.make_async_copy(ref, ref, recv.at[sem]).wait()

    def to_partner(cx, cy, low, high):
        pltpu.make_async_remote_copy(
            src_ref=part(cx, cy, low, high),
            dst_ref=part(cx, cy, low, high),
            send_sem=csend,
            recv_sem=crecv,
            device_id=partner,
            device_id_type=MESH,
        ).start()

    bounds = ((0, 3, 5), (5, 7, 10))

    def at(colour, i, j):
        return (xs[i], ys[j]) if colour == 0 else (xs[j], ys[i])

    peers = (((x_minus, x_plus), (y_minus, y_plus)), ((y_minus, y_plus), (x_minus, x_plus)))

    def sem_of(colour, stage, i, k):
        return colour * 20 + (k if stage == 0 else 4 + 4 * i + k)

    def start_ring(colour, stage, i):
        low, _, high = bounds[colour]
        minus, plus = peers[colour][stage]
        cx, cy = at(colour, i, 0)
        push(cx, cy, low, high, sem_of(colour, stage, place_there(i, stage), 0), plus)
        push(cx, cy, low, high, sem_of(colour, stage, place_there(i, stage), 1), minus)

    def place_there(i, stage):
        return i

    def step_ring(colour, stage, i, side):
        low, mid, high = bounds[colour]
        minus, plus = peers[colour][stage]
        cx, cy = at(colour, side, 0) if stage == 0 else at(colour, i, side)
        arrived(cx, cy, low, high, sem_of(colour, stage, i, side - 1))
        if side == 1:
            push(cx, cy, low, mid, sem_of(colour, stage, i, 2), plus)
        else:
            push(cx, cy, mid, high, sem_of(colour, stage, i, 3), minus)
        to_partner(cx, cy, low, high)

    def end_ring(colour, stage, i):
        low, mid, high = bounds[colour]
        cx, cy = at(colour, 3, 0) if stage == 0 else at(colour, i, 3)
        arrived(cx, cy, low, mid, sem_of(colour, stage, i, 2))
        arrived(cx, cy, mid, high, sem_of(colour, stage, i, 3))
        to_partner(cx, cy, low, high)

    for colour in range(2):
        start_ring(colour, 0, 0)
    for colour in range(2):
        start_ring(colour, 1, 0)
    for colour in range(2):
        low, _, high = bounds[colour]
        to_partner(x, y, low, high)
    for side in (1, 2):
        for colour in range(2):
            step_ring(colour, 0, 0, side)
            start_ring(colour, 1, side)
    for side in (1, 2):
        for colour in range(2):
            step_ring(colour, 1, 0, side)
    for colour in range(2):
        end_ring(colour, 0, 0)
        start_ring(colour, 1, 3)
    for i in (1, 2):
        for side in (1, 2):
            for colour in range(2):
                step_ring(colour, 1, i, side)
    for colour in range(2):
        end_ring(colour, 1, 0)
    for side in (1, 2):
        for colour in range(2):
            step_ring(colour, 1, 3, side)
    for i in (1, 2, 3):
        for colour in range(2):
            end_ring(colour, 1, i)

    for step in range(1, 8):
        for b in range(2):
            go, copy = z_copy(step, b)
            pl.when(go)(copy.wait_send)
    whole = g_ref.at[pl.ds(0, 15)]
    pltpu.make_async_copy(whole, whole, send).wait()
    whole = g_ref.at[pl.ds(0, 16)]
    pltpu.make_async_copy(whole, whole, csend).wait()
    pltpu.make_async_copy(whole, whole, crecv).wait()


def gather(day_ranks, confidence):
    shape = (PIECES, SLOTS, HALF, 2, 128)
    return pl.pallas_call(
        gather_kernel,
        out_shape=jax.ShapeDtypeStruct(shape, jnp.float32),
        in_specs=[pl.BlockSpec(memory_space=pltpu.VMEM)] * 2,
        out_specs=pl.BlockSpec(memory_space=pltpu.VMEM),
        scratch_shapes=[
            pltpu.VMEM((2, HALF, 2, 128), jnp.float32),
            pltpu.SemaphoreType.DMA((16,)),
            pltpu.SemaphoreType.DMA((SLOTS,)),
            pltpu.SemaphoreType.DMA((40,)),
            pltpu.SemaphoreType.DMA,
            pltpu.SemaphoreType.DMA,
            pltpu.SemaphoreType.DMA,
        ],
        compiler_params=pltpu.CompilerParams(
            collective_id=0, has_side_effects=True, vmem_limit_bytes=16 * 2**20
        ),
        name="gather",
    )(day_ranks, confidence)


def correlate_kernel(g_ref, out_ref, left, right, offset, mean_scale):
    step = pl.program_id(0)
    tm = lax.axis_index("tm")
    z = tm // 2
    rows = g_ref

    def load(block):
        lists = []
        for x_lo in range(2):
            base = (block * 2 + x_lo) * PART * 2
            halves = [rows[pl.ds(base + h, SEC // 2, 2), :] for h in range(2)]
            lists.append(jnp.concatenate(halves, 1))
        return jnp.concatenate(lists, 0)

    @pl.when(step == 0)
    def _():
        row = lax.broadcasted_iota(jnp.int32, (SEC, STOCKS), 0)
        x_lo = (row >= SEC // 2).astype(jnp.int32)
        inner = row - x_lo * (SEC // 2)
        local = (inner * 37) >> 8
        q = jnp.where(x_lo == 0, first_local(z, 0), first_local(z, 1)) + local
        day = HALF * (4 * (q >> 1) + 2 * x_lo + (q & 1)) + inner - HALF * local
        off = day - (LEAD + ENDS_DEV * tm)
        offset[...] = jnp.where(inner < PART, off, -1).astype(jnp.float32)
        right[3 * SEC :, :] = jnp.zeros((DEPTH - 3 * SEC, STOCKS), jnp.bfloat16)

    off = offset[...]

    def centred(block):
        values = load(block)
        common = (off >= ENDS_DEV - 1) & (off < WIN)
        centre = jnp.sum(jnp.where(common, values, 0.0), 0, keepdims=True) / (WIN - ENDS_DEV + 1)
        return jnp.where((off >= 0) & (off < SPAN), values - centre, 0.0)

    def moments(values):
        square = values * values
        out = []
        for e in range(ENDS_DEV):
            inside = (off >= e) & (off < e + WIN)
            mean = jnp.sum(jnp.where(inside, values, 0.0), 0, keepdims=True) / WIN
            power = jnp.sum(jnp.where(inside, square, 0.0), 0, keepdims=True) / WIN
            out.append((mean, lax.rsqrt(power - mean * mean + epsilon)))
        return out

    def split(values):
        high = values.astype(jnp.bfloat16)
        return high, (values - high.astype(jnp.float32)).astype(jnp.bfloat16)

    @pl.when(step == 0)
    def _():
        values = centred(lax.axis_index("asset"))
        for e, (mean, scale) in enumerate(moments(values)):
            inside = (off >= e) & (off < e + WIN)
            unit = jnp.where(inside, (values - mean) * (scale / WIN), 0.0)
            high, low = split(unit)
            zero = jnp.zeros((DEPTH - 3 * SEC, STOCKS), jnp.bfloat16)
            stacked = jnp.concatenate([high, high, low, zero], 0)
            left[e * STOCKS : (e + 1) * STOCKS, :] = stacked.T

    values = centred(step)
    high, low = split(values)
    right[0:SEC, :] = high
    right[SEC : 2 * SEC, :] = low
    right[2 * SEC : 3 * SEC, :] = high
    for e, (_, scale) in enumerate(moments(values)):
        gram = jnp.dot(
            left[e * STOCKS : (e + 1) * STOCKS, :],
            right[...],
            preferred_element_type=jnp.float32,
        )
        out_ref[e] = (gram * scale).astype(jnp.bfloat16)


def correlate(rows):
    return pl.pallas_call(
        correlate_kernel,
        grid=(BLOCKS,),
        out_shape=jax.ShapeDtypeStruct((ENDS_DEV, STOCKS, STOCKS * BLOCKS), jnp.bfloat16),
        in_specs=[pl.BlockSpec(memory_space=pltpu.VMEM)],
        out_specs=pl.BlockSpec((ENDS_DEV, STOCKS, STOCKS), lambda a: (0, 0, a)),
        scratch_shapes=[
            pltpu.VMEM((ENDS_DEV * STOCKS, DEPTH), jnp.bfloat16),
            pltpu.VMEM((DEPTH, STOCKS), jnp.bfloat16),
            pltpu.VMEM((SEC, STOCKS), jnp.float32),
            pltpu.VMEM((16, STOCKS), jnp.float32),
        ],
        compiler_params=pltpu.CompilerParams(vmem_limit_bytes=32 * 2**20),
        cost_estimate=pl.CostEstimate(
            flops=2 * 1536 * 4096 * 512, bytes_accessed=15 * 10**6, transcendentals=0
        ),
        name="correlate",
    )(rows)


def per_device(day_ranks, confidence):
    pieces = gather(day_ranks, confidence)
    return correlate(pieces.reshape(PIECES * PART * 2, 128))


def solution(mesh):
    return jax.shard_map(
        per_device,
        mesh=mesh,
        in_specs=(P("tm", "asset"), P("tm", "asset")),
        out_specs=P("tm", "asset", None),
        check_vma=False,
    )
```

time: 141 us -> 49.7 us (0.35)
  waiting for transfers between devices: 61.1 us -> 0 us
  Pallas kernels: 0 us -> 48 us
  matrix products: 21.3 us -> 0 us
  other arithmetic: 19.9 us -> 0 us
  between operations: 13.6 us -> 0.01 us
  local copies, waits for them, and re-layouts: 15 us -> 1.43 us
  starting transfers between devices: 10.1 us -> 0 us
    all_gather x1 -> x0, waiting for transfers between devices: 50.5 us -> none  [per_device(): lax.all_gather(own_span, 'asset', axis=1, tiled=True)]
    pallas_call x0 -> x2, Pallas kernels: none -> 48 us  [the longest x1 31.7 us: gather(): pl.pallas_call(gather_kernel, out_shape=jax.ShapeDtypeStruct(shape, jnp.f...]
    dot_general x6 -> x0, matrix products: 21.3 us -> none  [window_gram(): lax.dot_general(left_rows[start_index:stop_index], right_rows[start_index...]
    reduce_sum x4 -> x0, other arithmetic: 11.3 us -> none  [the longest x2 6.09 us: window_moments(): window_scale = lax.rsqrt(jnp.sum(centred * centred, 1) / WIN + epsilon)]
    unnamed x12 -> x4, local copies, waits for them, and re-layouts: 12.1 us -> 1.43 us
    all_to_all x1 -> x0, waiting for transfers between devices: 10.5 us -> none  [copy_for_each(): lax.all_to_all(jnp.broadcast_to(shard[None], (size, *shard.shape)), axis,...]
    all_to_all x1 -> x0, starting transfers between devices: 10 us -> none  [copy_for_each(): lax.all_to_all(jnp.broadcast_to(shard[None], (size, *shard.shape)), axis,...]
    convert_element_type x1 -> x0, other arithmetic: 7.76 us -> none  [cross_tile(): return ((gram_sums / WIN - centre) * spread).astype(jnp.bfloat16)]
  transfers between devices with their start and end apart: 2 -> 0, of which waited for: 2 -> 0; matrix products, arithmetic and copies ran while one was open for 0% -> 0% of each run, Pallas kernels for 0% -> 0%
where the time goes in v1:
time: 49.7 us; the launch traced here: 49.4 us
  Pallas kernels  48 us (97%)
  local copies, waits for them, and re-layouts  1.43 us (3%)
    pallas_call x1, Pallas kernels, gather(): pl.pallas_call(gather_kernel, out_shape=jax.ShapeDtypeStruct(shape, jnp.f...  31.7 us
    pallas_call x1, Pallas kernels, correlate(): pl.pallas_call(correlate_kernel, grid=(BLOCKS,), out_shape=jax.ShapeDtype...  16.3 us
    unnamed x4, local copies, waits for them, and re-layouts  1.43 us

profile of v1, /device:TPU:1, one launch (start us, length us, event | category | flops | bytes accessed | tf_op | source)
XLA Modules:
  0.0 49.4 jit_solution(17072831084981045506)
XLA Ops:
  0.0 0.0 copy-start
  0.0 0.7 %copy-done = s32[14,256]{1,0:T(8,128)S(1)} copy-done((s32[14,256]{1,0:T(8,128)S(1)}, s32[14,256]{1,0:T(8,128)}, u32[]{:S(2)}) %copy-start) | copy-done | bytes 14360
  0.7 0.0 copy-start.1
  0.7 0.7 %copy-done.1 = f32[14,256]{1,0:T(8,128)S(1)} copy-done((f32[14,256]{1,0:T(8,128)S(1)}, f32[14,256]{1,0:T(8,128)}, u32[]{:S(2)}) %copy-start.1) | copy-done | bytes 14360
  1.4 31.7 %gather.1 = f32[34,10,7,2,128]{4,3,2,1,0:T(2,128)S(1)} custom-call(s32[14,256]{1,0:T(8,128)S(1)} %copy-done, f32[14,256]{1,0:T(8,128)S(1)} %copy-done.1), custom_call_target="tpu_custom_call" | custom-call | tf_op jit(solution)/shard_map/gather/pallas_call | solution.py:211
  33.1 16.3 %correlate.1 = bf16[6,256,4096]{2,1,0:T(8,128)(2,1)} custom-call(f32[4760,128]{1,0:T(8,128)S(1)} %bitcast.1), custom_call_target="tpu_custom_call" | custom-call | flops 6442450944 | bytes 15000000 | tf_op jit(solution)/shard_map/correlate/pallas_call | solution.py:306
Async XLA Ops:
  0.0 0.7 %copy-start = (s32[14,256]{1,0:T(8,128)S(1)}, s32[14,256]{1,0:T(8,128)}, u32[]{:S(2)}) copy-start(s32[14,256]{1,0:T(8,128)} %ranks_ref.1) | copy-start | bytes 43012
  0.7 0.7 %copy-start.1 = (f32[14,256]{1,0:T(8,128)S(1)}, f32[14,256]{1,0:T(8,128)}, u32[]{:S(2)}) copy-start(f32[14,256]{1,0:T(8,128)} %conf_ref.1) | copy-start | bytes 43012
